TPU v7x, 32 devices: a whole 2x2x4 slice. The times are simulated.
32 devices in a mesh: row: 8 (over z, y), col: 4 (over x, core).
Axes of the slice: x: 2, y: 2, z: 4, core: 2. Of those that a mesh axis runs over, the one named last changes fastest.
Arguments:
- matrix: float32 [1536, 1536], P('row', 'col'), may hold values from -30 to 30
- panels: float32 [2, 1536, 256], P(None, ('col', 'row')), may hold values from -0.15625 to 0.15625
- factors: float32 [2, 256, 256], replicated, may hold values from -1 to 2, as said below
Outputs:
- reduced: float32 [1536, 1536], P('row', 'col')
Inputs may be any that keep to these rules, and one draw needn't show every extreme that they name: Each factors[s] is upper triangular with diagonal entries between 1 and 2.
All inputs are finite; a program needn't handle non-finite values.
Results may differ from a plain program's by a relative error of at most 0.0003.
Values sent between devices are 32-bit elements; how exact they have to be, the bound alone decides.
No kernel may reach another device: no remote copies, remote signals or barrier semaphores. Data moves between devices by JAX's collectives and lax.ppermute only.
A program may use at most 64 MiB of HBM per device.

v0:
```python
import jax
import jax.numpy as jnp
from jax import lax
from jax.sharding import PartitionSpec as P

highest = lax.Precision.HIGHEST


def from_root(block, axis, owner):
    block = jnp.where(lax.axis_index(axis) == owner, block, jnp.zeros_like(block))
    return lax.psum(block, axis)


def matmul(left, right):
    return jnp.dot(left, right, precision=highest, preferred_element_type=jnp.float32)


def transposed_product(left, right):
    return lax.dot_general(
        left, right, (((0,), (0,)), ((), ())), precision=highest, preferred_element_type=jnp.float32
    )


def outer_product(left, right):
    return lax.dot_general(
        left, right, (((1,), (1,)), ((), ())), precision=highest, preferred_element_type=jnp.float32
    )


def per_device(matrix, panels, factors):
    row_count = lax.axis_size("row")
    col_count = lax.axis_size("col")
    my_row = lax.axis_index("row")
    block_rows = matrix.shape[0]
    share = panels.shape[1]
    source = my_row * col_count // row_count
    offset = share * (my_row * col_count - source * row_count)
    gathered = lax.all_gather(panels, "row", axis=1, tiled=True)
    relayed = from_root(gathered, "col", source)
    current = matrix
    for section in range(panels.shape[0]):
        factor = factors[section]
        panel_cols = gathered[section]
        panel_rows = lax.dynamic_slice_in_dim(relayed[section], offset, block_rows, 0)
        sums_rows = lax.psum(matmul(current, panel_cols), "col")
        sums_cols = lax.psum(transposed_product(current, panel_rows), "row")
        image_rows = matmul(sums_rows, factor)
        image_cols = matmul(sums_cols, factor)
        inner = lax.psum(transposed_product(panel_rows, image_rows), "row")
        correction = transposed_product(factor, inner)
        update_rows = image_rows - 0.5 * matmul(panel_rows, correction)
        update_cols = image_cols - 0.5 * matmul(panel_cols, correction)
        current = (
            current
            - outer_product(panel_rows, update_cols)
            - outer_product(update_rows, panel_cols)
        )
    return current


def solution(mesh):
    return jax.shard_map(
        per_device,
        mesh=mesh,
        in_specs=(P("row", "col"), P(None, ("col", "row"), None), P()),
        out_specs=P("row", "col"),
        check_vma=False,
    )
```

profile of v0, /device:TPU:0, one launch (start us, length us, event | category | flops | bytes accessed | tf_op | source)
XLA Modules:
  0.0 285.3 jit_solution(409260807775912355)
XLA Ops:
  6.5 0.0 all-reduce.14.cloned.1.call-start
  6.5 0.0 copy-start.1
  6.5 34.2 %all_gather.3 = f32[2,384,256]{2,1,0:T(8,128)S(1)} all-gather(f32[2,48,256]{2,1,0:T(8,128)} %param.4), channel_id=1, replica_groups=mesh['row'=8,'col'=4] {'row'}, dimensions={1}, use_global_device_ids=true | all-gather | bytes 884736 | tf_op jit(solution)/shard_map/all_gather | solution.py:38
  40.8 0.0 copy-done.1
  40.8 1.2 fusion.4
  41.9 1.0 broadcast_select_fusion
  42.9 0.0 all-reduce.14.cloned.1.call-update
  42.9 0.0 all-reduce.12.cloned.1.call-start
  43.0 36.9 %all-reduce.14.cloned.1.call-done = (f32[192,256]{1,0:T(8,128)}, f32[2,384,256]{2,1,0:T(8,128)}) async-done(((f32[192,256]{1,0:T(8,128)}, f32[2,384,256]{2,1,0:T(8,128)}), (f32[192,256]{1,0:T(8,128)}, f32[2,384,256]{2,1,0:T(8,128)})) %all-reduce.14.cloned.1.call-update) | async-done | bytes 983056 | tf_op jit(solution)/shard_map/psum | solution.py:45
  79.9 0.0 copy-start
  79.9 0.0 copy-start.4
  79.9 1.2 fusion.49
  81.1 0.0 copy-done
  81.1 0.0 copy-done.4
  81.2 0.3 fusion.13
  81.5 1.4 convolution_bitcast_fusion
  82.9 1.4 fusion.30
  84.3 0.0 all-reduce.12.cloned.1.call-update
  84.3 0.0 all-reduce.8.cloned.1.call-start
  84.4 74.2 %all-reduce.12.cloned.1.call-done = (f32[256,256]{1,0:T(8,128)}, f32[384,256]{0,1:T(8,128)}) async-done(((f32[256,256]{1,0:T(8,128)}, f32[384,256]{0,1:T(8,128)}), (f32[256,256]{1,0:T(8,128)}, f32[384,256]{0,1:T(8,128)})) %all-reduce.12.cloned.1.call-update) | async-done | bytes 655376 | tf_op jit(solution)/shard_map/psum | solution.py:49
  158.6 1.5 fusion.11
  160.2 0.4 fusion.3
  160.6 0.0 copy-start.2
  160.6 0.5 fusion.1
  161.1 0.5 copy-done.2
  161.6 0.8 convolution_subtract_fusion.1
  162.4 0.5 convolution_subtract_fusion.5
  162.9 0.5 convolution_subtract_fusion.4
  163.5 1.2 fusion.5
  164.7 0.0 all-reduce.8.cloned.1.call-update
  164.7 0.0 all-reduce.10.cloned.1.call-start
  164.7 1.6 fusion.26
  166.3 30.0 %all-reduce.8.cloned.1.call-done = f32[192,256]{1,0:T(8,128)} async-done(((f32[192,256]{1,0:T(8,128)}), f32[192,256]{1,0:T(8,128)}) %all-reduce.8.cloned.1.call-update) | async-done | bytes 196624 | tf_op jit(solution)/shard_map/psum | solution.py:45
  196.4 1.3 fusion.8
  197.6 1.4 fusion.24
  199.0 0.0 all-reduce.10.cloned.1.call-update
  199.0 74.5 %all-reduce.10.cloned.1.call-done = (f32[256,256]{1,0:T(8,128)}, f32[384,256]{1,0:T(8,128)}) async-done(((f32[256,256]{1,0:T(8,128)}, f32[384,256]{1,0:T(8,128)}), (f32[256,256]{1,0:T(8,128)}, f32[384,256]{1,0:T(8,128)})) %all-reduce.10.cloned.1.call-update) | async-done | bytes 655376 | tf_op jit(solution)/shard_map/psum | solution.py:49
  273.5 1.5 fusion.6
  275.1 0.4 fusion.2
  275.5 0.0 copy-start.3
  275.5 0.5 fusion
  276.0 0.5 copy-done.3
  276.5 0.5 convolution_subtract_fusion
  277.0 0.5 convolution_subtract_fusion.3
  277.5 1.3 convolution_subtract_fusion.2
Async XLA Ops:
  6.5 73.3 %all-reduce.14.cloned.1.call-start = ((), (), s32[]{:S(2)}) async-start(), calls=%async_computation.3 | async-start | bytes 1966080 | tf_op jit(solution)/shard_map/psum | solution.py:45
  6.5 34.2 %copy-start.1 = (f32[192,384]{1,0:T(8,128)S(1)}, f32[192,384]{1,0:T(8,128)}, u32[]{:S(2)}) copy-start(f32[192,384]{1,0:T(8,128)} %param.3) | copy-start | bytes 884740
  42.9 115.7 %all-reduce.12.cloned.1.call-start = ((), (), s32[]{:S(2)}) async-start(), calls=%async_computation.2 | async-start | bytes 1310720 | tf_op jit(solution)/shard_map/psum | solution.py:49
  79.9 1.3 copy-start
  79.9 1.3 copy-start.4
  84.3 112.0 %all-reduce.8.cloned.1.call-start = ((), (), s32[]{:S(2)}) async-start(), calls=%async_computation | async-start | bytes 393216 | tf_op jit(solution)/shard_map/psum | solution.py:45
  160.6 1.0 copy-start.2
  164.7 108.8 %all-reduce.10.cloned.1.call-start = ((), (), s32[]{:S(2)}) async-start(), calls=%async_computation.1 | async-start | bytes 1310720 | tf_op jit(solution)/shard_map/psum | solution.py:49
  275.5 1.0 copy-start.3
Sparse Core Ops, SparseCore 0:
  43.0 36.7 all-reduce.13
  84.5 74.1 all-reduce.11
  164.8 31.5 all-reduce.7
  199.7 73.7 all-reduce.9
where the time goes:
time: 286 us; the launch traced here: 285 us
  waiting for transfers between devices  216 us (76%)
  blocking collectives  34.2 us (12%)
  matrix products  18.8 us (7%)
  between operations  13.3 us (5%)
    psum x2, waiting for transfers between devices, per_device(): inner = lax.psum(transposed_product(panel_rows, image_rows), 'row')  149 us
    psum x2, waiting for transfers between devices, per_device(): sums_rows = lax.psum(matmul(current, panel_cols), 'col')  66.9 us
    all_gather x1, blocking collectives, per_device(): gathered = lax.all_gather(panels, 'row', axis=1, tiled=True)  34.2 us
    dot_general x6, matrix products, transposed_product(): lax.dot_general(left, right, (((0,), (0,)), ((), ())), precision=highest,...  8.86 us
    dot_general x10, matrix products, matmul(): jnp.dot(left, right, precision=highest, preferred_element_type=jnp.float32)  7.09 us
  transfers between devices with their start and end apart: 4, of which 4 were waited for; matrix products, arithmetic and copies ran while one was open for 1% of the time, Pallas kernels for 0%

commit v1 on v0

--- a/solution.py
+++ b/solution.py
@@ -35,7 +35,12 @@
     share = panels.shape[1]
     source = my_row * col_count // row_count
     offset = share * (my_row * col_count - source * row_count)
-    gathered = lax.all_gather(panels, "row", axis=1, tiled=True)
+    ring = [panels]
+    for hop in range(7):
+        ring.append(lax.ppermute(ring[-1], "row", [(dev, (dev + 1) % 8) for dev in range(8)]))
+    gathered = jnp.roll(
+        jnp.concatenate(ring[::-1], axis=1), (lax.axis_index("row") + 1) * ring[0].shape[1], axis=1
+    )
     relayed = from_root(gathered, "col", source)
     current = matrix
     for section in range(panels.shape[0]):

time: 286 us -> 303 us (1.059)
  waiting for transfers between devices: 216 us -> 263 us
  blocking collectives: 34.2 us -> 0 us
  starting transfers between devices: 0.13 us -> 3.32 us
    ppermute x0 -> x7, waiting for transfers between devices: none -> 50.9 us  [per_device(): lax.ppermute(ring[-1], 'row', [(dev, (dev + 1) % 8) for dev in range(8)])]
    psum x2 -> x1, waiting for transfers between devices: 66.9 us -> 29.7 us  [per_device(): sums_rows = lax.psum(matmul(current, panel_cols), 'col')]
    all_gather x1 -> x0, blocking collectives: 34.2 us -> none  [per_device(): gathered = lax.all_gather(panels, 'row', axis=1, tiled=True)]
    psum x2 -> x3, waiting for transfers between devices: 149 us -> 183 us  [the longest x2 149 us: per_device(): sums_cols = lax.psum(transposed_product(current, panel_rows), 'row')]
  transfers between devices with their start and end apart: 4 -> 11, of which waited for: 4 -> 11; matrix products, arithmetic and copies ran while one was open for 1% -> 1% of each run, Pallas kernels for 0% -> 0%
where the time goes in v1:
time: 303 us
  waiting for transfers between devices  263 us (87%)
  matrix products  19.6 us (6%)
  between operations  13.4 us (4%)
  starting transfers between devices  3.32 us (1%)
    psum x2, waiting for transfers between devices, per_device(): sums_cols = lax.psum(transposed_product(current, panel_rows), 'row')  149 us
    ppermute x7, waiting for transfers between devices, per_device(): lax.ppermute(ring[-1], 'row', [(dev, (dev + 1) % 8) for dev in range(8)])  50.9 us
    psum x1, waiting for transfers between devices, from_root(): return lax.psum(block, axis)  33.7 us
    psum x1, waiting for transfers between devices, per_device(): sums_rows = lax.psum(matmul(current, panel_cols), 'col')  29.7 us
    dot_general x6, matrix products, transposed_product(): lax.dot_general(left, right, (((0,), (0,)), ((), ())), precision=highest,...  8.96 us
    dot_general x10, matrix products, matmul(): jnp.dot(left, right, precision=highest, preferred_element_type=jnp.float32)  7.72 us
  transfers between devices with their start and end apart: 11, of which 11 were waited for; matrix products, arithmetic and copies ran while one was open for 1% of the time, Pallas kernels for 0%

profile of v1, /device:TPU:0, one launch (start us, length us, event | category | flops | bytes accessed | tf_op | source)
XLA Modules:
  0.0 302.8 jit_solution(14281005762350813719)
XLA Ops:
  6.5 0.0 copy-start.2
  6.5 0.0 all-reduce.14.cloned.1.call-start
  6.5 3.0 collective-permute-start
  9.5 6.1 %collective-permute-done = f32[2,48,256]{2,1,0:T(8,128)S(1)} collective-permute-done((f32[2,48,256]{2,1,0:T(8,128)}, f32[2,48,256]{2,1,0:T(8,128)S(1)}, u32[]{:S(2)}, u32[]{:S(2)}) %collective-permute-start) | collective-permute-done | bytes 98336 | tf_op jit(solution)/shard_map/ppermute | solution.py:40
  15.6 0.0 collective-permute-start.1
  15.6 7.3 %collective-permute-done.1 = f32[2,48,256]{2,1,0:T(8,128)S(1)} collective-permute-done((f32[2,48,256]{2,1,0:T(8,128)S(1)}, f32[2,48,256]{2,1,0:T(8,128)S(1)}, u32[]{:S(2)}, u32[]{:S(2)}) %collective-permute-start.1) | collective-permute-done | bytes 98336 | tf_op jit(solution)/shard_map/ppermute | solution.py:40
  23.0 0.0 collective-permute-start.2
  23.0 7.3 %collective-permute-done.2 = f32[2,48,256]{2,1,0:T(8,128)S(1)} collective-permute-done((f32[2,48,256]{2,1,0:T(8,128)S(1)}, f32[2,48,256]{2,1,0:T(8,128)S(1)}, u32[]{:S(2)}, u32[]{:S(2)}) %collective-permute-start.2) | collective-permute-done | bytes 98336 | tf_op jit(solution)/shard_map/ppermute | solution.py:40
  30.3 0.0 collective-permute-start.3
  30.3 7.3 %collective-permute-done.3 = f32[2,48,256]{2,1,0:T(8,128)S(1)} collective-permute-done((f32[2,48,256]{2,1,0:T(8,128)S(1)}, f32[2,48,256]{2,1,0:T(8,128)S(1)}, u32[]{:S(2)}, u32[]{:S(2)}) %collective-permute-start.3) | collective-permute-done | bytes 98336 | tf_op jit(solution)/shard_map/ppermute | solution.py:40
  37.6 0.0 collective-permute-start.4
  37.6 7.4 %collective-permute-done.4 = f32[2,48,256]{2,1,0:T(8,128)S(1)} collective-permute-done((f32[2,48,256]{2,1,0:T(8,128)S(1)}, f32[2,48,256]{2,1,0:T(8,128)S(1)}, u32[]{:S(2)}, u32[]{:S(2)}) %collective-permute-start.4) | collective-permute-done | bytes 98336 | tf_op jit(solution)/shard_map/ppermute | solution.py:40
  44.9 0.0 collective-permute-start.5
  44.9 8.2 %collective-permute-done.5 = f32[2,48,256]{2,1,0:T(8,128)S(1)} collective-permute-done((f32[2,48,256]{2,1,0:T(8,128)S(1)}, f32[2,48,256]{2,1,0:T(8,128)S(1)}, u32[]{:S(2)}, u32[]{:S(2)}) %collective-permute-start.5) | collective-permute-done | bytes 98336 | tf_op jit(solution)/shard_map/ppermute | solution.py:40
  53.2 0.0 collective-permute-start.6
  53.2 7.3 %collective-permute-done.6 = f32[2,48,256]{2,1,0:T(8,128)S(1)} collective-permute-done((f32[2,48,256]{2,1,0:T(8,128)S(1)}, f32[2,48,256]{2,1,0:T(8,128)S(1)}, u32[]{:S(2)}, u32[]{:S(2)}) %collective-permute-start.6) | collective-permute-done | bytes 98336 | tf_op jit(solution)/shard_map/ppermute | solution.py:40
  60.6 0.9 constant_dynamic-update-slice_fusion.8
  61.5 0.0 copy-start.1
  61.6 0.0 copy-done.2
  61.7 1.0 dynamic-slice_select_fusion
  62.7 0.0 copy-done.1
  62.7 0.0 copy-start
  62.7 1.5 convolution_bitcast_fusion.1
  64.2 0.0 all-reduce.14.cloned.1.call-update
  64.2 0.0 all-reduce.12.cloned.1.call-start
  64.3 33.7 %all-reduce.14.cloned.1.call-done = (f32[2,384,256]{2,1,0:T(8,128)}, f32[192,256]{0,1:T(8,128)}) async-done(((f32[2,384,256]{2,1,0:T(8,128)}, f32[192,256]{0,1:T(8,128)}), (f32[2,384,256]{2,1,0:T(8,128)}, f32[192,256]{0,1:T(8,128)})) %all-reduce.14.cloned.1.call-update) | async-done | bytes 983056 | tf_op jit(solution)/shard_map/psum | solution.py:11
  97.9 0.0 copy-start.5
  97.9 1.2 fusion.56
  99.1 0.0 copy-done
  99.1 0.0 copy-done.5
  99.2 0.6 fusion.13
  99.7 1.4 convolution_bitcast_fusion
  101.2 1.4 fusion.31
  102.5 0.0 all-reduce.12.cloned.1.call-update
  102.5 0.0 all-reduce.8.cloned.1.call-start
  102.6 74.4 %all-reduce.12.cloned.1.call-done = (f32[384,256]{0,1:T(8,128)}, f32[256,256]{1,0:T(8,128)}) async-done(((f32[384,256]{0,1:T(8,128)}, f32[256,256]{1,0:T(8,128)}), (f32[384,256]{0,1:T(8,128)}, f32[256,256]{1,0:T(8,128)})) %all-reduce.12.cloned.1.call-update) | async-done | bytes 655376 | tf_op jit(solution)/shard_map/psum | solution.py:51
  177.0 0.0 copy-start.3
  177.0 1.6 fusion.11
  178.6 0.4 fusion.3
  179.0 0.0 copy-done.3
  179.0 0.8 fusion.15
  179.8 0.5 fusion
  180.4 0.5 convolution_subtract_fusion.3
  180.9 0.6 convolution_subtract_fusion.2
  181.5 1.2 fusion.4
  182.7 0.0 all-reduce.8.cloned.1.call-update
  182.7 0.2 all-reduce.10.cloned.1.call-start
  182.9 1.6 fusion.27
  184.5 29.7 %all-reduce.8.cloned.1.call-done = f32[192,256]{1,0:T(8,128)} async-done(((f32[192,256]{1,0:T(8,128)}), f32[192,256]{1,0:T(8,128)}) %all-reduce.8.cloned.1.call-update) | async-done | bytes 196624 | tf_op jit(solution)/shard_map/psum | solution.py:50
  214.2 1.3 fusion.7
  215.5 1.4 fusion.25
  216.9 0.0 all-reduce.10.cloned.1.call-update
  216.9 74.5 %all-reduce.10.cloned.1.call-done = (f32[384,256]{1,0:T(8,128)}, f32[256,256]{1,0:T(8,128)}) async-done(((f32[384,256]{1,0:T(8,128)}, f32[256,256]{1,0:T(8,128)}), (f32[384,256]{1,0:T(8,128)}, f32[256,256]{1,0:T(8,128)})) %all-reduce.10.cloned.1.call-update) | async-done | bytes 655376 | tf_op jit(solution)/shard_map/psum | solution.py:51
  291.4 0.0 copy-start.4
  291.4 1.6 fusion.5
  293.0 0.4 fusion.2
  293.4 0.0 copy-done.4
  293.5 0.5 fusion.9
  293.9 0.5 fusion.1
  294.5 0.5 convolution_subtract_fusion.1
  295.0 1.3 convolution_subtract_fusion
  (15 shorter events, 0.1 us)
Async XLA Ops:
  6.5 55.1 %copy-start.2 = (f32[2,48,256]{2,1,0:T(8,128)S(1)}, f32[2,48,256]{2,1,0:T(8,128)}, u32[]{:S(2)}) copy-start(f32[2,48,256]{2,1,0:T(8,128)} %param.4) | copy-start | bytes 294916
  6.5 91.4 %all-reduce.14.cloned.1.call-start = ((), (), s32[]{:S(2)}) async-start(), calls=%async_computation.3 | async-start | bytes 2097152 | tf_op jit(solution)/shard_map/psum | solution.py:11
  6.5 9.1 %collective-permute-start = (f32[2,48,256]{2,1,0:T(8,128)}, f32[2,48,256]{2,1,0:T(8,128)S(1)}, u32[]{:S(2)}, u32[]{:S(2)}) collective-permute-start(f32[2,48,256]{2,1,0:T(8,128)} %param.4), channel_id=1, source_target_pairs={{0,4},{4,8},{8,12},{12,16},{16,20},{20,24},{24,28},{28,0},{1,5},{5... | collective-permute-start | bytes 294920 | tf_op jit(solution)/shard_map/ppermute | solution.py:40
  15.6 7.3 %collective-permute-start.1 = (f32[2,48,256]{2,1,0:T(8,128)S(1)}, f32[2,48,256]{2,1,0:T(8,128)S(1)}, u32[]{:S(2)}, u32[]{:S(2)}) collective-permute-start(f32[2,48,256]{2,1,0:T(8,128)S(1)} %collective-permute-done), channel_id=1, source_target_pairs={{0,4},{4,8},{8,12},{12,16},{16,20},{20,24},{24,28},{28,0},{1,5},{5... | collective-permute-start | bytes 294920 | tf_op jit(solution)/shard_map/ppermute | solution.py:40
  23.0 7.3 %collective-permute-start.2 = (f32[2,48,256]{2,1,0:T(8,128)S(1)}, f32[2,48,256]{2,1,0:T(8,128)S(1)}, u32[]{:S(2)}, u32[]{:S(2)}) collective-permute-start(f32[2,48,256]{2,1,0:T(8,128)S(1)} %collective-permute-done.1), channel_id=1, source_target_pairs={{0,4},{4,8},{8,12},{12,16},{16,20},{20,24},{24,28},{28,0},{1,5},{5... | collective-permute-start | bytes 294920 | tf_op jit(solution)/shard_map/ppermute | solution.py:40
  30.3 7.3 %collective-permute-start.3 = (f32[2,48,256]{2,1,0:T(8,128)S(1)}, f32[2,48,256]{2,1,0:T(8,128)S(1)}, u32[]{:S(2)}, u32[]{:S(2)}) collective-permute-start(f32[2,48,256]{2,1,0:T(8,128)S(1)} %collective-permute-done.2), channel_id=1, source_target_pairs={{0,4},{4,8},{8,12},{12,16},{16,20},{20,24},{24,28},{28,0},{1,5},{5... | collective-permute-start | bytes 294920 | tf_op jit(solution)/shard_map/ppermute | solution.py:40
  37.6 7.4 %collective-permute-start.4 = (f32[2,48,256]{2,1,0:T(8,128)S(1)}, f32[2,48,256]{2,1,0:T(8,128)S(1)}, u32[]{:S(2)}, u32[]{:S(2)}) collective-permute-start(f32[2,48,256]{2,1,0:T(8,128)S(1)} %collective-permute-done.3), channel_id=1, source_target_pairs={{0,4},{4,8},{8,12},{12,16},{16,20},{20,24},{24,28},{28,0},{1,5},{5... | collective-permute-start | bytes 294920 | tf_op jit(solution)/shard_map/ppermute | solution.py:40
  44.9 8.2 %collective-permute-start.5 = (f32[2,48,256]{2,1,0:T(8,128)S(1)}, f32[2,48,256]{2,1,0:T(8,128)S(1)}, u32[]{:S(2)}, u32[]{:S(2)}) collective-permute-start(f32[2,48,256]{2,1,0:T(8,128)S(1)} %collective-permute-done.4), channel_id=1, source_target_pairs={{0,4},{4,8},{8,12},{12,16},{16,20},{20,24},{24,28},{28,0},{1,5},{5... | collective-permute-start | bytes 294920 | tf_op jit(solution)/shard_map/ppermute | solution.py:40
  53.2 7.3 %collective-permute-start.6 = (f32[2,48,256]{2,1,0:T(8,128)S(1)}, f32[2,48,256]{2,1,0:T(8,128)S(1)}, u32[]{:S(2)}, u32[]{:S(2)}) collective-permute-start(f32[2,48,256]{2,1,0:T(8,128)S(1)} %collective-permute-done.5), channel_id=1, source_target_pairs={{0,4},{4,8},{8,12},{12,16},{16,20},{20,24},{24,28},{28,0},{1,5},{5... | collective-permute-start | bytes 294920 | tf_op jit(solution)/shard_map/ppermute | solution.py:40
  61.5 1.2 copy-start.1
  62.7 36.5 %copy-start = (f32[2,256,256]{2,1,0:T(8,128)S(1)}, f32[2,256,256]{2,1,0:T(8,128)}, u32[]{:S(2)}) copy-start(f32[2,256,256]{2,1,0:T(8,128)} %param.5) | copy-start | bytes 1572868
  64.2 112.8 %all-reduce.12.cloned.1.call-start = ((), (), s32[]{:S(2)}) async-start(), calls=%async_computation.2 | async-start | bytes 1310720 | tf_op jit(solution)/shard_map/psum | solution.py:51
  97.9 1.2 copy-start.5
  102.5 111.7 %all-reduce.8.cloned.1.call-start = ((), (), s32[]{:S(2)}) async-start(), calls=%async_computation | async-start | bytes 393216 | tf_op jit(solution)/shard_map/psum | solution.py:50
  177.0 2.0 copy-start.3
  182.7 108.7 %all-reduce.10.cloned.1.call-start = ((), (), s32[]{:S(2)}) async-start(), calls=%async_computation.1 | async-start | bytes 1310720 | tf_op jit(solution)/shard_map/psum | solution.py:51
  291.4 2.0 copy-start.4
Sparse Core Ops, SparseCore 0:
  64.3 33.5 all-reduce.13
  102.7 74.2 all-reduce.11
  182.8 31.3 all-reduce.7
  217.6 73.7 all-reduce.9

commit v2 on v0

--- a/solution.py
+++ b/solution.py
@@ -42,7 +42,7 @@
         factor = factors[section]
         panel_cols = gathered[section]
         panel_rows = lax.dynamic_slice_in_dim(relayed[section], offset, block_rows, 0)
-        sums_rows = lax.psum(matmul(current, panel_cols), "col")
+        sums_rows = jnp.sum(lax.all_gather(matmul(current, panel_cols), "col"), axis=0)
         sums_cols = lax.psum(transposed_product(current, panel_rows), "row")
         image_rows = matmul(sums_rows, factor)
         image_cols = matmul(sums_cols, factor)

time: 286 us -> 258 us (0.902)
  waiting for transfers between devices: 216 us -> 170 us
  blocking collectives: 34.2 us -> 52.6 us
    psum x2 -> x1, waiting for transfers between devices: 66.9 us -> 23.9 us  [from_root(): return lax.psum(block, axis)]
    all_gather x0 -> x2, blocking collectives: none -> 18.5 us  [per_device(): lax.all_gather(matmul(current, panel_cols), 'col')]
  transfers between devices with their start and end apart: 4 -> 3, of which waited for: 4 -> 3; matrix products, arithmetic and copies ran while one was open for 1% -> 0% of each run, Pallas kernels for 0% -> 0%
where the time goes in v2:
time: 258 us
  waiting for transfers between devices  170 us (66%)
  blocking collectives  52.6 us (20%)
  matrix products  16.5 us (6%)
  between operations  13.3 us (5%)
  local copies, waits for them, and re-layouts  3.97 us (2%)
    psum x2, waiting for transfers between devices, per_device(): inner = lax.psum(transposed_product(panel_rows, image_rows), 'row')  146 us
    all_gather x1, blocking collectives, per_device(): gathered = lax.all_gather(panels, 'row', axis=1, tiled=True)  34.1 us
    psum x1, waiting for transfers between devices, from_root(): return lax.psum(block, axis)  23.9 us
    all_gather x2, blocking collectives, per_device(): lax.all_gather(matmul(current, panel_cols), 'col')  18.5 us
    dot_general x6, matrix products, transposed_product(): lax.dot_general(left, right, (((0,), (0,)), ((), ())), precision=highest,...  8.86 us
  transfers between devices with their start and end apart: 3, of which 3 were waited for; matrix products, arithmetic and copies ran while one was open for 0% of the time, Pallas kernels for 0%

profile of v2, /device:TPU:0, one launch (start us, length us, event | category | flops | bytes accessed | tf_op | source)
XLA Modules:
  0.0 257.9 jit_solution(14440347683205914332)
XLA Ops:
  6.5 0.0 all-reduce.6.cloned.1.call-start
  6.5 34.1 %all_gather.15 = f32[2,384,256]{2,1,0:T(8,128)S(1)} all-gather(f32[2,48,256]{2,1,0:T(8,128)} %param.4), channel_id=1, replica_groups=mesh['row'=8,'col'=4] {'row'}, dimensions={1}, use_global_device_ids=true | all-gather | bytes 884736 | tf_op jit(solution)/shard_map/all_gather | solution.py:38
  40.6 0.9 broadcast_select_fusion
  41.6 0.0 copy-start.1
  41.6 0.0 all-reduce.6.cloned.1.call-update
  41.6 0.0 all-reduce.10.cloned.1.call-start
  41.6 0.9 copy-done.1
  42.5 0.5 fusion.4
  43.0 9.9 %all-gather = f32[768,256]{1,0:T(8,128)S(1)} all-gather(f32[192,256]{1,0:T(8,128)S(1)} %fusion.4), channel_id=2, replica_groups=mesh['row'=8,'col'=4] {'col'}, dimensions={0}, use_global_device_ids=true | all-gather | bytes 983040 | tf_op jit(solution)/shard_map/all_gather | solution.py:45
  53.0 0.0 copy-start
  53.0 0.1 reduce_sum.18
  53.0 1.0 copy-done
  54.0 0.3 fusion.13
  54.3 23.9 %all-reduce.6.cloned.1.call-done = f32[2,384,256]{2,1,0:T(8,128)} async-done(((f32[2,384,256]{2,1,0:T(8,128)}), f32[2,384,256]{2,1,0:T(8,128)}) %all-reduce.6.cloned.1.call-update) | async-done | bytes 786448 | tf_op jit(solution)/shard_map/psum | solution.py:11
  78.3 1.2 fusion.49
  79.4 1.4 convolution_bitcast_fusion
  80.9 1.4 fusion.30
  82.2 0.0 all-reduce.10.cloned.1.call-update
  82.2 0.0 all-reduce.8.cloned.1.call-start
  82.3 73.9 %all-reduce.10.cloned.1.call-done = (f32[256,256]{1,0:T(8,128)}, f32[384,256]{0,1:T(8,128)}) async-done(((f32[256,256]{1,0:T(8,128)}, f32[384,256]{0,1:T(8,128)}), (f32[256,256]{1,0:T(8,128)}, f32[384,256]{0,1:T(8,128)})) %all-reduce.10.cloned.1.call-update) | async-done | bytes 655376 | tf_op jit(solution)/shard_map/psum | solution.py:49
  156.2 1.5 fusion.11
  157.7 0.4 fusion.3
  158.2 0.0 copy-start.2
  158.2 0.5 fusion.1
  158.7 0.5 copy-done.2
  159.2 0.8 convolution_subtract_fusion.1
  160.0 0.5 convolution_subtract_fusion.5
  160.5 0.5 convolution_subtract_fusion.4
  161.1 0.5 fusion.5
  161.6 1.6 fusion.26
  163.2 8.6 %all-gather.1 = f32[768,256]{1,0:T(8,128)S(1)} all-gather(f32[192,256]{1,0:T(8,128)S(1)} %fusion.5), channel_id=3, replica_groups=mesh['row'=8,'col'=4] {'col'}, dimensions={0}, use_global_device_ids=true | all-gather | bytes 983040 | tf_op jit(solution)/shard_map/all_gather | solution.py:45
  171.7 0.1 reduce_sum.19
  171.8 0.3 fusion.8
  172.1 1.4 fusion.24
  173.5 0.0 all-reduce.8.cloned.1.call-update
  173.5 72.6 %all-reduce.8.cloned.1.call-done = (f32[256,256]{1,0:T(8,128)}, f32[384,256]{1,0:T(8,128)}) async-done(((f32[256,256]{1,0:T(8,128)}, f32[384,256]{1,0:T(8,128)}), (f32[256,256]{1,0:T(8,128)}, f32[384,256]{1,0:T(8,128)})) %all-reduce.8.cloned.1.call-update) | async-done | bytes 655376 | tf_op jit(solution)/shard_map/psum | solution.py:49
  246.1 1.5 fusion.6
  247.6 0.4 fusion.2
  248.1 0.0 copy-start.3
  248.1 0.5 fusion
  248.6 0.5 copy-done.3
  249.1 0.5 convolution_subtract_fusion
  249.6 0.5 convolution_subtract_fusion.3
  250.1 1.3 convolution_subtract_fusion.2
Async XLA Ops:
  6.5 71.7 %all-reduce.6.cloned.1.call-start = ((), (), s32[]{:S(2)}) async-start(), calls=%async_computation | async-start | bytes 1572864 | tf_op jit(solution)/shard_map/psum | solution.py:11
  41.6 1.0 copy-start.1
  41.6 114.6 %all-reduce.10.cloned.1.call-start = ((), (), s32[]{:S(2)}) async-start(), calls=%async_computation.2 | async-start | bytes 1310720 | tf_op jit(solution)/shard_map/psum | solution.py:49
  53.0 1.0 copy-start
  82.2 163.8 %all-reduce.8.cloned.1.call-start = ((), (), s32[]{:S(2)}) async-start(), calls=%async_computation.1 | async-start | bytes 1310720 | tf_op jit(solution)/shard_map/psum | solution.py:49
  158.2 1.0 copy-start.2
  248.1 1.0 copy-start.3
Sparse Core Ops, SparseCore 0:
  41.7 36.5 all-reduce.5
  82.4 73.7 all-reduce.9
  173.7 72.3 all-reduce.7
